TPU v7x, 32 devices: a whole 2x2x4 slice. The times are simulated.
32 devices in a mesh: win: 16 (over z, y, core), head: 2 (over x).
Axes of the slice: x: 2, y: 2, z: 4, core: 2. Of those that a mesh axis runs over, the one named last changes fastest.
Arguments:
- qkv: bfloat16 [3, 16, 96, 48, 1024], P(None, 'win', 'head'), may hold values from -10 to 10
Outputs:
- attended: bfloat16 [16, 96, 48, 1024], P('win', 'head')
All inputs are finite; a program needn't handle non-finite values.
Results may differ from a plain program's by a relative error of at most 0.0047.
Values may be sent and summed in bfloat16 or wider, within the bound.
A program may use at most 192 MiB of HBM per device.

v0:
```python
import math
import jax
import jax.numpy as jnp
from jax import lax
from jax.sharding import PartitionSpec as P

HEAD_DIM = 128


def from_behind(shard, axis, by):
    count = lax.axis_size(axis)
    return lax.ppermute(shard, axis, [(i, (i + by) % count) for i in range(count)])


def partner(value, axis, apart):
    mask = 2**apart
    pairs = [(source, source ^ mask) for source in range(lax.axis_size(axis))]
    return lax.ppermute(value, axis, pairs)


def attend(queries, keys, values, labels_query, labels_key):
    query_count, head_count, head_width = queries.shape
    block_rows = math.gcd(query_count, 576)
    score_scale = 1.0 / math.sqrt(head_width)

    def one_block(pieces):
        query_block, label_block = pieces
        scores = (
            jnp.einsum("qhd,khd->hqk", query_block, keys, preferred_element_type=jnp.float32)
            * score_scale
        )
        allowed = label_block[:, None] == labels_key[None, :]
        scores = jnp.where(allowed[None], scores, -jnp.inf)
        row_max = jnp.max(scores, axis=-1, keepdims=True)
        weights = jnp.exp(scores - row_max)
        row_total = jnp.sum(weights, axis=-1, keepdims=True)
        mixture = jnp.einsum(
            "hqk,khd->qhd", weights.astype(jnp.bfloat16), values, preferred_element_type=jnp.float32
        )
        return (mixture / jnp.transpose(row_total, (1, 0, 2))).astype(jnp.bfloat16)

    query_blocks = queries.reshape(query_count // block_rows, block_rows, head_count, head_width)
    label_blocks = labels_query.reshape(query_count // block_rows, block_rows)
    return lax.map(one_block, (query_blocks, label_blocks)).reshape(
        query_count, head_count, head_width
    )


def window_attention(window, labels):
    row_count, side_cells, channels = (window.shape[1], window.shape[2], window.shape[3])
    head_count = channels // HEAD_DIM
    window_parts = window.reshape(
        3, row_count // side_cells, side_cells * side_cells, head_count, HEAD_DIM
    )
    label_parts = labels.reshape(row_count // side_cells, side_cells * side_cells)
    outputs = []
    for window_row in range(row_count // side_cells):
        outputs.append(
            attend(
                window_parts[0, window_row],
                window_parts[1, window_row],
                window_parts[2, window_row],
                label_parts[window_row],
                label_parts[window_row],
            )
        )
    return jnp.stack(outputs).reshape(row_count, side_cells, channels)


def body(qkv):
    side_cells = qkv.shape[3]
    half_cols = side_cells // 2
    tokens = qkv[:, 0]
    arrived = from_behind(tokens[:, :, :half_cols], "win", -2)
    tokens = jnp.concatenate([tokens[:, :, half_cols:], arrived], axis=2)
    head_view = lax.all_to_all(tokens, "head", split_axis=3, concat_axis=1, tiled=True)
    half_rows = head_view.shape[1]
    crossing = partner(head_view[:, :half_cols], "win", 0)
    extended = jnp.concatenate([head_view[:, half_cols:], crossing], axis=1)
    lat_half = lax.axis_index("win") % 2
    row_index = jnp.arange(half_rows, dtype=jnp.int32)[:, None]
    wrapped = jnp.logical_and(lat_half == 1, row_index >= half_rows - half_cols)
    labels = jnp.broadcast_to(jnp.where(wrapped, 1, 0).astype(jnp.int32), (half_rows, side_cells))
    result = window_attention(extended, labels)
    returned = partner(result[half_rows - half_cols :], "win", 0)
    row_fixed = jnp.concatenate([returned, result[: half_rows - half_cols]], axis=0)
    restored = lax.all_to_all(row_fixed, "head", split_axis=0, concat_axis=2, tiled=True)
    from_west = from_behind(restored[:, half_cols:], "win", 2)
    restored = jnp.concatenate([from_west, restored[:, :half_cols]], axis=1)
    return restored[None]


def solution(mesh):
    in_specs = (P(None, "win", "head", None, None),)
    out_specs = P("win", "head", None, None)
    return jax.shard_map(body, mesh=mesh, in_specs=in_specs, out_specs=out_specs, check_vma=False)
```

profile of v0, /device:TPU:0, one launch (start us, length us, event | category | flops | bytes accessed | tf_op | source)
XLA Modules:
  0.0 1056.7 jit_solution(9154201426480805091)
XLA Ops:
  0.0 6.6 fusion.44
  6.6 6.1 collective-permute-start
  12.7 151.6 %collective-permute-done = bf16[3,48,24,1024]{3,2,1,0:T(8,128)(2,1)S(1)} collective-permute-done((bf16[3,48,24,1024]{3,2,1,0:T(8,128)(2,1)S(1)}, bf16[3,48,24,1024]{3,2,1,0:T(8,128)(2,1)S(1)}, u32[]{:S(2)}, u32[]{:S(2)}) %collective-permute-start) | collective-permute-done | bytes 7077920 | tf_op jit(solution)/shard_map/ppermute | solution.py:12
  164.3 6.7 pad_maximum_fusion
  171.0 42.0 %copy.38 = bf16[3,48,48,1024]{2,1,0,3:T(8,128)(2,1)} copy(bf16[3,48,48,1024]{3,2,1,0:T(8,128)(2,1)} %pad_maximum_fusion) | data formatting | bytes 28311552 | tf_op jit(solution)/shard_map/concatenate | solution.py:75
  213.1 66.4 %reshape.117 = bf16[2,2,1769472]{2,1,0:T(2,128)(2,1)} reshape(bf16[1024,3,48,48]{3,2,1,0:T(8,128)(2,1)} %bitcast.107) | data formatting | bytes 28311552
  279.5 169.9 %all_to_all.36 = bf16[2,2,1769472]{2,1,0:T(2,128)(2,1)} all-to-all(bf16[2,2,1769472]{2,1,0:T(2,128)(2,1)} %reshape.117), channel_id=1, replica_groups=mesh['win'=16,'head'=2] {'head'}, dimensions={0} | all-to-all | bytes 28311552 | tf_op jit(solution)/shard_map/all_to_all | solution.py:76
  449.4 57.7 %reshape.118 = bf16[1024,3,48,48]{3,2,1,0:T(8,128)(2,1)} reshape(bf16[2,2,1769472]{2,1,0:T(2,128)(2,1)} %all_to_all.36) | data formatting | bytes 28311552
  507.1 59.6 %copy.52 = bf16[3,48,48,2,512]{4,3,2,1,0:T(2,128)(2,1)} copy(bf16[3,48,48,2,512]{2,1,0,4,3:T(8,128)(2,1)} %bitcast.108) | data formatting | bytes 28311552 | tf_op jit(solution)/shard_map/all_to_all | solution.py:76
  566.7 9.2 copy.40
  576.0 5.0 copy-done
  589.9 5.5 slice.94
  595.4 8.2 pad_maximum_fusion.1
  603.6 20.3 %reshape.99 = bf16[3,2,2304,4,128]{4,3,2,1,0:T(4,128)(2,1)} reshape(bf16[3,96,48,512]{3,2,1,0:T(8,128)(2,1)} %pad_maximum_fusion.1) | data formatting | bytes 28311552 | tf_op jit(solution)/shard_map/reshape | solution.py:52
  623.9 11.5 %slice_bitcast_fusion.2 = (bf16[2304,4,128]{2,1,0:T(4,128)(2,1)S(1)}, bf16[2304,4,128]{2,1,0:T(4,128)(2,1)}, bf16[2304,4,128]{2,1,0:T(4,128)(2,1)}, bf16[1,1,230...) fusion(bf16[3,2,2304,4,128]{4,3,2,1,0:T(4,128)(2,1)} %reshape.99), kind=kLoop, calls=%fused_computation.45 | loop fusion | bytes 28311552 | tf_op jit(solution)/shard_map/squeeze | solution.py:62
  639.4 131.7 %while.22 = (s32[]{:T(128)}, bf16[4,576,4,128]{3,1,0,2:T(8,128)(2,1)}, s32[4,576]{1,0:T(4,128)S(1)}, bf16[4,576,4,128]{3,2,1,0:T(4,128)(2,1)}, bf16[2304,4,128]{...) while((s32[]{:T(128)}, ...), condition=%wide.region_3.4_spmd.clone, body=%wide.region_0.3_spmd.clone.sunk | while | flops 2778213888 | bytes 85615160 | solution.py:44
  641.7 9.5 fusion.65
  651.2 10.6 %fusion.66 = f32[4,576]{1,0:T(4,128)S(1)} fusion(f32[4,576,2304]{2,1,0:T(8,128)} %get-tuple-element.309, f32[4,576]{1,0:T(4,128)S(1)} %get-tuple-element.310, pred[576,2304]{1,0:T(8,128)(4,1)S(1)} %broadcast_compare_fusion.4), kind=kLoop, calls=%fused_computation.5.clone.1 | loop fusion | flops 21231360 | bytes 22579200 | tf_op jit(solution)/shard_map/while/body/eval_jaxpr/reduce_sum | solution.py:36
  661.9 10.5 fusion.67
  674.6 9.5 fusion.65
  684.2 10.6 %fusion.66 = f32[4,576]{1,0:T(4,128)S(1)} fusion(f32[4,576,2304]{2,1,0:T(8,128)} %get-tuple-element.309, f32[4,576]{1,0:T(4,128)S(1)} %get-tuple-element.310, pred[576,2304]{1,0:T(8,128)(4,1)S(1)} %broadcast_compare_fusion.4), kind=kLoop, calls=%fused_computation.5.clone.1 | loop fusion | flops 21231360 | bytes 22579200 | tf_op jit(solution)/shard_map/while/body/eval_jaxpr/reduce_sum | solution.py:36
  694.8 10.5 fusion.67
  707.5 9.5 fusion.65
  717.1 10.6 %fusion.66 = f32[4,576]{1,0:T(4,128)S(1)} fusion(f32[4,576,2304]{2,1,0:T(8,128)} %get-tuple-element.309, f32[4,576]{1,0:T(4,128)S(1)} %get-tuple-element.310, pred[576,2304]{1,0:T(8,128)(4,1)S(1)} %broadcast_compare_fusion.4), kind=kLoop, calls=%fused_computation.5.clone.1 | loop fusion | flops 21231360 | bytes 22579200 | tf_op jit(solution)/shard_map/while/body/eval_jaxpr/reduce_sum | solution.py:36
  727.7 10.5 fusion.67
  740.5 9.5 fusion.65
  750.0 10.6 %fusion.66 = f32[4,576]{1,0:T(4,128)S(1)} fusion(f32[4,576,2304]{2,1,0:T(8,128)} %get-tuple-element.309, f32[4,576]{1,0:T(4,128)S(1)} %get-tuple-element.310, pred[576,2304]{1,0:T(8,128)(4,1)S(1)} %broadcast_compare_fusion.4), kind=kLoop, calls=%fused_computation.5.clone.1 | loop fusion | flops 21231360 | bytes 22579200 | tf_op jit(solution)/shard_map/while/body/eval_jaxpr/reduce_sum | solution.py:36
  760.7 10.5 fusion.67
  777.1 134.7 %while.23 = (s32[]{:T(128)}, bf16[4,576,4,128]{3,1,0,2:T(8,128)(2,1)}, s32[4,576]{1,0:T(4,128)}, bf16[4,576,4,128]{3,2,1,0:T(4,128)(2,1)}, bf16[2304,4,128]{2,0,...) while((s32[]{:T(128)}, bf16[4,576,4,128]{3,1,0,2:T(8,128)(2,1)}, ...), condition=%wide.region_7.8_spmd.clone, body=%wide.region_4.7_spmd.clone.sunk | while | flops 2778213888 | bytes 85615160 | solution.py:44
  780.4 9.5 fusion.71
  789.9 10.6 %fusion.72 = f32[4,576]{1,0:T(4,128)S(1)} fusion(f32[4,576,2304]{2,1,0:T(8,128)} %get-tuple-element.318, f32[4,576]{1,0:T(4,128)S(1)} %get-tuple-element.319, pred[576,2304]{1,0:T(8,128)(4,1)S(1)} %broadcast_compare_fusion.5), kind=kLoop, calls=%fused_computation.23.clone.1 | loop fusion | flops 21231360 | bytes 22579200 | tf_op jit(solution)/shard_map/while/body/eval_jaxpr/reduce_sum | solution.py:36
  800.6 10.4 fusion.73
  814.0 9.5 fusion.71
  823.5 10.6 %fusion.72 = f32[4,576]{1,0:T(4,128)S(1)} fusion(f32[4,576,2304]{2,1,0:T(8,128)} %get-tuple-element.318, f32[4,576]{1,0:T(4,128)S(1)} %get-tuple-element.319, pred[576,2304]{1,0:T(8,128)(4,1)S(1)} %broadcast_compare_fusion.5), kind=kLoop, calls=%fused_computation.23.clone.1 | loop fusion | flops 21231360 | bytes 22579200 | tf_op jit(solution)/shard_map/while/body/eval_jaxpr/reduce_sum | solution.py:36
  834.2 10.4 fusion.73
  847.6 9.5 fusion.71
  857.1 10.6 %fusion.72 = f32[4,576]{1,0:T(4,128)S(1)} fusion(f32[4,576,2304]{2,1,0:T(8,128)} %get-tuple-element.318, f32[4,576]{1,0:T(4,128)S(1)} %get-tuple-element.319, pred[576,2304]{1,0:T(8,128)(4,1)S(1)} %broadcast_compare_fusion.5), kind=kLoop, calls=%fused_computation.23.clone.1 | loop fusion | flops 21231360 | bytes 22579200 | tf_op jit(solution)/shard_map/while/body/eval_jaxpr/reduce_sum | solution.py:36
  867.8 10.4 fusion.73
  881.2 9.5 fusion.71
  890.8 10.6 %fusion.72 = f32[4,576]{1,0:T(4,128)S(1)} fusion(f32[4,576,2304]{2,1,0:T(8,128)} %get-tuple-element.318, f32[4,576]{1,0:T(4,128)S(1)} %get-tuple-element.319, pred[576,2304]{1,0:T(8,128)(4,1)S(1)} %broadcast_compare_fusion.5), kind=kLoop, calls=%fused_computation.23.clone.1 | loop fusion | flops 21231360 | bytes 22579200 | tf_op jit(solution)/shard_map/while/body/eval_jaxpr/reduce_sum | solution.py:36
  901.4 10.4 fusion.73
  911.9 2.8 pad_maximum_fusion.2
  914.7 12.0 %copy.50 = bf16[2,2304,4,128]{3,2,1,0:T(4,128)(2,1)} copy(bf16[2,2304,4,128]{3,1,2,0:T(8,128)(2,1)S(1)} %pad_maximum_fusion.2) | data formatting | bytes 9437184 | tf_op jit(solution)/shard_map/stack | solution.py:67
  926.7 8.0 reshape.100
  936.8 2.5 collective-permute-done.2
  939.7 56.5 %all_to_all.37 = bf16[96,48,512]{2,1,0:T(8,128)(2,1)S(1)} all-to-all(bf16[96,48,512]{2,1,0:T(8,128)(2,1)S(1)} %pad_maximum_fusion.3), channel_id=1, replica_groups=mesh['win'=16,'head'=2] {'head'}, dimensions={0} | all-to-all | bytes 9437184 | tf_op jit(solution)/shard_map/all_to_all | solution.py:87
  997.7 55.8 %collective-permute-done.3 = bf16[48,24,1024]{2,1,0:T(8,128)(2,1)S(1)} collective-permute-done((bf16[48,24,1024]{2,1,0:T(8,128)(2,1)S(1)}, bf16[48,24,1024]{2,1,0:T(8,128)(2,1)S(1)}, u32[]{:S(2)}, u32[]{:S(2)}) %collective-permute-start.3) | collective-permute-done | bytes 2359328 | tf_op jit(solution)/shard_map/ppermute | solution.py:12
  1053.5 2.7 maximum_bitcast_fusion
  (86 shorter events, 43.7 us)
Async XLA Ops:
  6.6 157.7 %collective-permute-start = (bf16[3,48,24,1024]{3,2,1,0:T(8,128)(2,1)S(1)}, bf16[3,48,24,1024]{3,2,1,0:T(8,128)(2,1)S(1)}, u32[]{:S(2)}, u32[]{:S(2)}) collective-permute-start(bf16[3,48,24,1024]{3,2,1,0:T(8,128)(2,1)S(1)} %get-tuple-element.219), channel_id=1, source_target_pairs={{0,28},{2,30},{4,0},{6,2},{8,4},{10,6},{12,8},{14,10},{16,12},{18,... | collective-permute-start | bytes 21233672 | tf_op jit(solution)/shard_map/ppermute | solution.py:12
  576.0 5.1 copy-start
  583.0 12.4 %collective-permute-start.1 = (bf16[3,24,48,512]{3,2,1,0:T(8,128)(2,1)}, bf16[3,24,48,512]{3,2,1,0:T(8,128)(2,1)S(1)}, u32[]{:S(2)}, u32[]{:S(2)}) collective-permute-start(bf16[3,24,48,512]{3,2,1,0:T(8,128)(2,1)} %slice.95), channel_id=1, source_target_pairs={{0,2},{2,0},{4,6},{6,4},{8,10},{10,8},{12,14},{14,12},{16,18},{18,... | collective-permute-start | bytes 10616840 | tf_op jit(solution)/shard_map/ppermute | solution.py:18
  651.2 10.7 %copy-start.3 = (bf16[2304,4,128]{2,0,1:T(8,128)(2,1)S(1)}, bf16[2304,4,128]{2,0,1:T(8,128)(2,1)}, u32[]{:S(2)}) copy-start(bf16[2304,4,128]{2,0,1:T(8,128)(2,1)} %get-tuple-element.365) | copy-start | bytes 7077892 | tf_op jit(solution)/shard_map/while
  684.1 10.7 %copy-start.3 = (bf16[2304,4,128]{2,0,1:T(8,128)(2,1)S(1)}, bf16[2304,4,128]{2,0,1:T(8,128)(2,1)}, u32[]{:S(2)}) copy-start(bf16[2304,4,128]{2,0,1:T(8,128)(2,1)} %get-tuple-element.365) | copy-start | bytes 7077892 | tf_op jit(solution)/shard_map/while
  717.1 10.7 %copy-start.3 = (bf16[2304,4,128]{2,0,1:T(8,128)(2,1)S(1)}, bf16[2304,4,128]{2,0,1:T(8,128)(2,1)}, u32[]{:S(2)}) copy-start(bf16[2304,4,128]{2,0,1:T(8,128)(2,1)} %get-tuple-element.365) | copy-start | bytes 7077892 | tf_op jit(solution)/shard_map/while
  750.0 10.7 %copy-start.3 = (bf16[2304,4,128]{2,0,1:T(8,128)(2,1)S(1)}, bf16[2304,4,128]{2,0,1:T(8,128)(2,1)}, u32[]{:S(2)}) copy-start(bf16[2304,4,128]{2,0,1:T(8,128)(2,1)} %get-tuple-element.365) | copy-start | bytes 7077892 | tf_op jit(solution)/shard_map/while
  771.1 2.4 copy-start.1
  773.2 3.9 copy-start.4
  789.9 10.7 %copy-start.2 = (bf16[2304,4,128]{2,0,1:T(8,128)(2,1)S(1)}, bf16[2304,4,128]{2,0,1:T(8,128)(2,1)}, u32[]{:S(2)}) copy-start(bf16[2304,4,128]{2,0,1:T(8,128)(2,1)} %get-tuple-element.341) | copy-start | bytes 7077892 | tf_op jit(solution)/shard_map/while
  823.5 10.7 %copy-start.2 = (bf16[2304,4,128]{2,0,1:T(8,128)(2,1)S(1)}, bf16[2304,4,128]{2,0,1:T(8,128)(2,1)}, u32[]{:S(2)}) copy-start(bf16[2304,4,128]{2,0,1:T(8,128)(2,1)} %get-tuple-element.341) | copy-start | bytes 7077892 | tf_op jit(solution)/shard_map/while
  857.1 10.7 %copy-start.2 = (bf16[2304,4,128]{2,0,1:T(8,128)(2,1)S(1)}, bf16[2304,4,128]{2,0,1:T(8,128)(2,1)}, u32[]{:S(2)}) copy-start(bf16[2304,4,128]{2,0,1:T(8,128)(2,1)} %get-tuple-element.341) | copy-start | bytes 7077892 | tf_op jit(solution)/shard_map/while
  890.8 10.7 %copy-start.2 = (bf16[2304,4,128]{2,0,1:T(8,128)(2,1)S(1)}, bf16[2304,4,128]{2,0,1:T(8,128)(2,1)}, u32[]{:S(2)}) copy-start(bf16[2304,4,128]{2,0,1:T(8,128)(2,1)} %get-tuple-element.341) | copy-start | bytes 7077892 | tf_op jit(solution)/shard_map/while
  934.7 4.6 slice-start
  936.2 3.0 collective-permute-start.2
  997.3 56.2 %collective-permute-start.3 = (bf16[48,24,1024]{2,1,0:T(8,128)(2,1)S(1)}, bf16[48,24,1024]{2,1,0:T(8,128)(2,1)S(1)}, u32[]{:S(2)}, u32[]{:S(2)}) collective-permute-start(bf16[48,24,1024]{2,1,0:T(8,128)(2,1)S(1)} %get-tuple-element.220), channel_id=1, source_target_pairs={{0,4},{2,6},{4,8},{6,10},{8,12},{10,14},{12,16},{14,18},{16,20},{1... | collective-permute-start | bytes 7077896 | tf_op jit(solution)/shard_map/ppermute | solution.py:12
where the time goes:
time: 1070 us; the launch traced here: 1060 us
  local copies, waits for them, and re-layouts  340 us (32%)
  blocking collectives  226 us (21%)
  waiting for transfers between devices  210 us (20%)
  matrix products  160 us (15%)
  other arithmetic  112 us (10%)
    ppermute x2, waiting for transfers between devices, from_behind(): lax.ppermute(shard, axis, [(i, (i + by) % count) for i in range(count)])  207 us
    all_to_all x1, blocking collectives, body(): lax.all_to_all(tokens, 'head', split_axis=3, concat_axis=1, tiled=True)  170 us
    unnamed x12, local copies, waits for them, and re-layouts  135 us
    reduce_sum x8, other arithmetic, one_block(): row_total = jnp.sum(weights, axis=-1, keepdims=True)  85.1 us
    dot_general x8, matrix products, one_block(): jnp.einsum('hqk,khd->qhd', weights.astype(jnp.bfloat16), values, preferre...  83.6 us
    dot_general x8, matrix products, one_block(): jnp.einsum('qhd,khd->hqk', query_block, keys, preferred_element_type=jnp....  76.4 us
    all_to_all x2, local copies, waits for them, and re-layouts, body(): lax.all_to_all(tokens, 'head', split_axis=3, concat_axis=1, tiled=True)  68.8 us
    all_to_all x1, blocking collectives, body(): lax.all_to_all(row_fixed, 'head', split_axis=0, concat_axis=2, tiled=True)  56.5 us
  transfers between devices with their start and end apart: 4, of which 3 were waited for; matrix products, arithmetic and copies ran while one was open for 1% of the time, Pallas kernels for 0%

commit v1 on v0

--- a/solution.py
+++ b/solution.py
@@ -73,7 +73,9 @@
     tokens = qkv[:, 0]
     arrived = from_behind(tokens[:, :, :half_cols], "win", -2)
     tokens = jnp.concatenate([tokens[:, :, half_cols:], arrived], axis=2)
-    head_view = lax.all_to_all(tokens, "head", split_axis=3, concat_axis=1, tiled=True)
+    cells = jnp.split(tokens, lax.axis_size("head"), axis=3)
+    received = lax.all_to_all(jnp.stack(cells), "head", 0, 0)
+    head_view = jnp.concatenate(received, axis=1)
     half_rows = head_view.shape[1]
     crossing = partner(head_view[:, :half_cols], "win", 0)
     extended = jnp.concatenate([head_view[:, half_cols:], crossing], axis=1)

time: 1070 us -> 809 us (0.76); the launches traced: 1060 us -> 807 us
  local copies, waits for them, and re-layouts: 340 us -> 107 us
  blocking collectives: 226 us -> 214 us
    unnamed x12 -> x10, local copies, waits for them, and re-layouts: 135 us -> 11.3 us
    all_to_all x2 -> x1, local copies, waits for them, and re-layouts: 68.8 us -> 2.47 us  [body(): received = lax.all_to_all(jnp.stack(cells), 'head', 0, 0)]
    concatenate x1 -> x0, local copies, waits for them, and re-layouts: 42 us -> none  [body(): tokens = jnp.concatenate([tokens[:, :, half_cols:], arrived], axis=2)]
    all_to_all x1, blocking collectives: 170 us -> 157 us  [body(): received = lax.all_to_all(jnp.stack(cells), 'head', 0, 0)]
  transfers between devices with their start and end apart: 4 -> 4, of which waited for: 3 -> 3; matrix products, arithmetic and copies ran while one was open for 1% -> 2% of each run, Pallas kernels for 0% -> 0%
where the time goes in v1:
time: 809 us; the launch traced here: 807 us
  blocking collectives  214 us (26%)
  waiting for transfers between devices  210 us (26%)
  matrix products  160 us (20%)
  other arithmetic  109 us (13%)
  local copies, waits for them, and re-layouts  107 us (13%)
    ppermute x2, waiting for transfers between devices, from_behind(): lax.ppermute(shard, axis, [(i, (i + by) % count) for i in range(count)])  207 us
    all_to_all x1, blocking collectives, body(): received = lax.all_to_all(jnp.stack(cells), 'head', 0, 0)  157 us
    reduce_sum x8, other arithmetic, one_block(): row_total = jnp.sum(weights, axis=-1, keepdims=True)  85.1 us
    dot_general x8, matrix products, one_block(): jnp.einsum('hqk,khd->qhd', weights.astype(jnp.bfloat16), values, preferre...  83.6 us
    dot_general x8, matrix products, one_block(): jnp.einsum('qhd,khd->hqk', query_block, keys, preferred_element_type=jnp....  76.4 us
    all_to_all x1, blocking collectives, body(): lax.all_to_all(row_fixed, 'head', split_axis=0, concat_axis=2, tiled=True)  56.5 us
    reshape x1, local copies, waits for them, and re-layouts, window_attention(): window.reshape(3, row_count // side_cells, side_cells * side_cells, head_...  20.3 us
  transfers between devices with their start and end apart: 4, of which 3 were waited for; matrix products, arithmetic and copies ran while one was open for 2% of the time, Pallas kernels for 0%

profile of v1, /device:TPU:0, one launch (start us, length us, event | category | flops | bytes accessed | tf_op | source)
XLA Modules:
  0.0 806.7 jit_solution(11438084062621293780)
XLA Ops:
  0.0 6.1 fusion.47
  6.1 6.1 collective-permute-start
  12.2 151.6 %collective-permute-done = bf16[3,48,24,1024]{3,2,1,0:T(8,128)(2,1)S(1)} collective-permute-done((bf16[3,48,24,1024]{3,2,1,0:T(8,128)(2,1)S(1)}, bf16[3,48,24,1024]{3,2,1,0:T(8,128)(2,1)S(1)}, u32[]{:S(2)}, u32[]{:S(2)}) %collective-permute-start) | collective-permute-done | bytes 7077920 | tf_op jit(solution)/shard_map/ppermute | solution.py:12
  163.8 1.9 fusion.45
  167.3 157.1 %all_to_all.23 = bf16[2,3,48,48,512]{4,3,2,1,0:T(8,128)(2,1)S(1)} all-to-all(bf16[2,3,48,48,512]{4,3,2,1,0:T(8,128)(2,1)S(1)} %pad_maximum_fusion), channel_id=1, replica_groups=mesh['win'=16,'head'=2] {'head'}, dimensions={0} | all-to-all | bytes 28311552 | tf_op jit(solution)/shard_map/all_to_all | solution.py:77
  324.4 2.5 copy.25
  326.8 5.0 copy-done
  331.9 2.0 slice.95
  340.8 5.5 slice.94
  346.3 8.2 %pad_maximum_fusion.1 = bf16[3,96,48,512]{3,2,1,0:T(8,128)(2,1)} fusion(bf16[3,24,48,512]{3,2,1,0:T(8,128)(2,1)S(1)} %collective-permute-done.1, bf16[3,72,48,512]{3,2,1,0:T(8,128)(2,1)S(1)} %slice.94), kind=kLoop, calls=%fused_computation.41 | loop fusion | flops 7077888 | bytes 28311552 | tf_op jit(solution)/shard_map/concatenate | solution.py:81
  354.5 20.3 %reshape.107 = bf16[3,2,2304,4,128]{4,3,2,1,0:T(4,128)(2,1)} reshape(bf16[3,96,48,512]{3,2,1,0:T(8,128)(2,1)} %pad_maximum_fusion.1) | data formatting | bytes 28311552 | tf_op jit(solution)/shard_map/reshape | solution.py:52
  374.8 11.3 %slice_bitcast_fusion.2 = (bf16[2304,4,128]{2,1,0:T(4,128)(2,1)S(1)}, bf16[2304,4,128]{2,1,0:T(4,128)(2,1)}, bf16[2304,4,128]{2,1,0:T(4,128)(2,1)}, bf16[1,1,230...) fusion(bf16[3,2,2304,4,128]{4,3,2,1,0:T(4,128)(2,1)} %reshape.107), kind=kLoop, calls=%fused_computation.51 | loop fusion | bytes 28311552 | tf_op jit(solution)/shard_map/squeeze | solution.py:62
  388.2 1.9 broadcast.86.clone2.1
  390.1 131.7 %while.22 = (s32[]{:T(128)}, bf16[4,576,4,128]{3,1,0,2:T(8,128)(2,1)}, s32[4,576]{1,0:T(4,128)S(1)}, bf16[4,576,4,128]{3,2,1,0:T(4,128)(2,1)}, bf16[2304,4,128]{...) while((s32[]{:T(128)}, ...), condition=%wide.region_3.4_spmd.clone, body=%wide.region_0.3_spmd.clone.sunk | while | flops 2778213888 | bytes 85615160 | solution.py:44
  392.4 9.5 %fusion.68 = (f32[4,576]{1,0:T(4,128)S(1)}, f32[4,576,2304]{2,1,0:T(8,128)}) fusion(pred[576,2304]{1,0:T(8,128)(4,1)S(1)} %broadcast_compare_fusion.4, bf16[2304,4,128]{2,0,1:T(8,128)(2,1)S(1)} %get-tuple-element.352, bf16[1,576,4,128]{3,2,1,0:T(4,128)(2,1)S(1)} %constant_dynamic-slice_fusion.4), kind=kOutput, calls=%fused_computation.4.clone.1 | convolution fusion | flops 1374877440 | bytes 25519104 | tf_op jit(solution)/shard_map/while/body/eval_jaxpr/qhd,khd->hqk/dot_general | solution.py:29
  401.9 10.6 %fusion.69 = f32[4,576]{1,0:T(4,128)S(1)} fusion(f32[4,576,2304]{2,1,0:T(8,128)} %get-tuple-element.297, f32[4,576]{1,0:T(4,128)S(1)} %get-tuple-element.298, pred[576,2304]{1,0:T(8,128)(4,1)S(1)} %broadcast_compare_fusion.4), kind=kLoop, calls=%fused_computation.5.clone.1 | loop fusion | flops 21231360 | bytes 22579200 | tf_op jit(solution)/shard_map/while/body/eval_jaxpr/reduce_sum | solution.py:36
  412.6 10.4 %fusion.70 = bf16[4,576,4,128]{3,1,0,2:T(8,128)(2,1)} fusion(bf16[4,576,4,128]{3,1,0,2:T(8,128)(2,1)} %get-tuple-element.341, s32[]{:T(128)} %get-tuple-element.340, bf16[2304,4,128]{2,0,1:T(8,128)(2,1)S(1)} %copy-done.3, f32[4,576,2304]{2,1,0:T(8,128)} %get-tuple-element.297, f32[4,576]{1,0:T(4,128)S(1)} %get-tuple-element.298, ...), kind=kOutput, calls=%fused_computation.13.clone.1 | convolution fusion | flops 1380777984 | bytes 25528832 | tf_op jit(solution)/shard_map/while/body/eval_jaxpr/hqk,khd->qhd/dot_general | solution.py:37
  425.3 9.5 %fusion.68 = (f32[4,576]{1,0:T(4,128)S(1)}, f32[4,576,2304]{2,1,0:T(8,128)}) fusion(pred[576,2304]{1,0:T(8,128)(4,1)S(1)} %broadcast_compare_fusion.4, bf16[2304,4,128]{2,0,1:T(8,128)(2,1)S(1)} %get-tuple-element.352, bf16[1,576,4,128]{3,2,1,0:T(4,128)(2,1)S(1)} %constant_dynamic-slice_fusion.4), kind=kOutput, calls=%fused_computation.4.clone.1 | convolution fusion | flops 1374877440 | bytes 25519104 | tf_op jit(solution)/shard_map/while/body/eval_jaxpr/qhd,khd->hqk/dot_general | solution.py:29
  434.8 10.6 %fusion.69 = f32[4,576]{1,0:T(4,128)S(1)} fusion(f32[4,576,2304]{2,1,0:T(8,128)} %get-tuple-element.297, f32[4,576]{1,0:T(4,128)S(1)} %get-tuple-element.298, pred[576,2304]{1,0:T(8,128)(4,1)S(1)} %broadcast_compare_fusion.4), kind=kLoop, calls=%fused_computation.5.clone.1 | loop fusion | flops 21231360 | bytes 22579200 | tf_op jit(solution)/shard_map/while/body/eval_jaxpr/reduce_sum | solution.py:36
  445.5 10.5 %fusion.70 = bf16[4,576,4,128]{3,1,0,2:T(8,128)(2,1)} fusion(bf16[4,576,4,128]{3,1,0,2:T(8,128)(2,1)} %get-tuple-element.341, s32[]{:T(128)} %get-tuple-element.340, bf16[2304,4,128]{2,0,1:T(8,128)(2,1)S(1)} %copy-done.3, f32[4,576,2304]{2,1,0:T(8,128)} %get-tuple-element.297, f32[4,576]{1,0:T(4,128)S(1)} %get-tuple-element.298, ...), kind=kOutput, calls=%fused_computation.13.clone.1 | convolution fusion | flops 1380777984 | bytes 25528832 | tf_op jit(solution)/shard_map/while/body/eval_jaxpr/hqk,khd->qhd/dot_general | solution.py:37
  458.2 9.5 %fusion.68 = (f32[4,576]{1,0:T(4,128)S(1)}, f32[4,576,2304]{2,1,0:T(8,128)}) fusion(pred[576,2304]{1,0:T(8,128)(4,1)S(1)} %broadcast_compare_fusion.4, bf16[2304,4,128]{2,0,1:T(8,128)(2,1)S(1)} %get-tuple-element.352, bf16[1,576,4,128]{3,2,1,0:T(4,128)(2,1)S(1)} %constant_dynamic-slice_fusion.4), kind=kOutput, calls=%fused_computation.4.clone.1 | convolution fusion | flops 1374877440 | bytes 25519104 | tf_op jit(solution)/shard_map/while/body/eval_jaxpr/qhd,khd->hqk/dot_general | solution.py:29
  467.8 10.6 %fusion.69 = f32[4,576]{1,0:T(4,128)S(1)} fusion(f32[4,576,2304]{2,1,0:T(8,128)} %get-tuple-element.297, f32[4,576]{1,0:T(4,128)S(1)} %get-tuple-element.298, pred[576,2304]{1,0:T(8,128)(4,1)S(1)} %broadcast_compare_fusion.4), kind=kLoop, calls=%fused_computation.5.clone.1 | loop fusion | flops 21231360 | bytes 22579200 | tf_op jit(solution)/shard_map/while/body/eval_jaxpr/reduce_sum | solution.py:36
  478.4 10.5 %fusion.70 = bf16[4,576,4,128]{3,1,0,2:T(8,128)(2,1)} fusion(bf16[4,576,4,128]{3,1,0,2:T(8,128)(2,1)} %get-tuple-element.341, s32[]{:T(128)} %get-tuple-element.340, bf16[2304,4,128]{2,0,1:T(8,128)(2,1)S(1)} %copy-done.3, f32[4,576,2304]{2,1,0:T(8,128)} %get-tuple-element.297, f32[4,576]{1,0:T(4,128)S(1)} %get-tuple-element.298, ...), kind=kOutput, calls=%fused_computation.13.clone.1 | convolution fusion | flops 1380777984 | bytes 25528832 | tf_op jit(solution)/shard_map/while/body/eval_jaxpr/hqk,khd->qhd/dot_general | solution.py:37
  491.2 9.5 %fusion.68 = (f32[4,576]{1,0:T(4,128)S(1)}, f32[4,576,2304]{2,1,0:T(8,128)}) fusion(pred[576,2304]{1,0:T(8,128)(4,1)S(1)} %broadcast_compare_fusion.4, bf16[2304,4,128]{2,0,1:T(8,128)(2,1)S(1)} %get-tuple-element.352, bf16[1,576,4,128]{3,2,1,0:T(4,128)(2,1)S(1)} %constant_dynamic-slice_fusion.4), kind=kOutput, calls=%fused_computation.4.clone.1 | convolution fusion | flops 1374877440 | bytes 25519104 | tf_op jit(solution)/shard_map/while/body/eval_jaxpr/qhd,khd->hqk/dot_general | solution.py:29
  500.7 10.6 %fusion.69 = f32[4,576]{1,0:T(4,128)S(1)} fusion(f32[4,576,2304]{2,1,0:T(8,128)} %get-tuple-element.297, f32[4,576]{1,0:T(4,128)S(1)} %get-tuple-element.298, pred[576,2304]{1,0:T(8,128)(4,1)S(1)} %broadcast_compare_fusion.4), kind=kLoop, calls=%fused_computation.5.clone.1 | loop fusion | flops 21231360 | bytes 22579200 | tf_op jit(solution)/shard_map/while/body/eval_jaxpr/reduce_sum | solution.py:36
  511.4 10.5 %fusion.70 = bf16[4,576,4,128]{3,1,0,2:T(8,128)(2,1)} fusion(bf16[4,576,4,128]{3,1,0,2:T(8,128)(2,1)} %get-tuple-element.341, s32[]{:T(128)} %get-tuple-element.340, bf16[2304,4,128]{2,0,1:T(8,128)(2,1)S(1)} %copy-done.3, f32[4,576,2304]{2,1,0:T(8,128)} %get-tuple-element.297, f32[4,576]{1,0:T(4,128)S(1)} %get-tuple-element.298, ...), kind=kOutput, calls=%fused_computation.13.clone.1 | convolution fusion | flops 1380777984 | bytes 25528832 | tf_op jit(solution)/shard_map/while/body/eval_jaxpr/hqk,khd->qhd/dot_general | solution.py:37
  521.8 2.1 copy.32
  526.0 1.9 broadcast.86.clone2
  527.8 134.5 %while.23 = (s32[]{:T(128)}, bf16[4,576,4,128]{3,1,0,2:T(8,128)(2,1)}, s32[4,576]{1,0:T(4,128)}, bf16[4,576,4,128]{3,2,1,0:T(4,128)(2,1)}, bf16[2304,4,128]{2,0,...) while((s32[]{:T(128)}, bf16[4,576,4,128]{3,1,0,2:T(8,128)(2,1)}, ...), condition=%wide.region_7.8_spmd.clone, body=%wide.region_4.7_spmd.clone.sunk | while | flops 2778213888 | bytes 85615160 | solution.py:44
  530.8 9.5 %fusion.74 = (f32[4,576]{1,0:T(4,128)S(1)}, f32[4,576,2304]{2,1,0:T(8,128)}) fusion(pred[576,2304]{1,0:T(8,128)(4,1)S(1)} %broadcast_compare_fusion.5, bf16[2304,4,128]{2,0,1:T(8,128)(2,1)S(1)} %get-tuple-element.328, bf16[1,576,4,128]{3,2,1,0:T(4,128)(2,1)S(1)} %constant_dynamic-slice_fusion.5), kind=kOutput, calls=%fused_computation.22.clone.1 | convolution fusion | flops 1374877440 | bytes 25519104 | tf_op jit(solution)/shard_map/while/body/eval_jaxpr/qhd,khd->hqk/dot_general | solution.py:29
  540.4 10.6 %fusion.75 = f32[4,576]{1,0:T(4,128)S(1)} fusion(f32[4,576,2304]{2,1,0:T(8,128)} %get-tuple-element.306, f32[4,576]{1,0:T(4,128)S(1)} %get-tuple-element.307, pred[576,2304]{1,0:T(8,128)(4,1)S(1)} %broadcast_compare_fusion.5), kind=kLoop, calls=%fused_computation.23.clone.1 | loop fusion | flops 21231360 | bytes 22579200 | tf_op jit(solution)/shard_map/while/body/eval_jaxpr/reduce_sum | solution.py:36
  551.0 10.4 %fusion.76 = bf16[4,576,4,128]{3,1,0,2:T(8,128)(2,1)} fusion(bf16[4,576,4,128]{3,1,0,2:T(8,128)(2,1)} %get-tuple-element.317, s32[]{:T(128)} %get-tuple-element.316, bf16[2304,4,128]{2,0,1:T(8,128)(2,1)S(1)} %copy-done.2, f32[4,576,2304]{2,1,0:T(8,128)} %get-tuple-element.306, f32[4,576]{1,0:T(4,128)S(1)} %get-tuple-element.307, ...), kind=kOutput, calls=%fused_computation.31.clone.1 | convolution fusion | flops 1380777984 | bytes 25528832 | tf_op jit(solution)/shard_map/while/body/eval_jaxpr/hqk,khd->qhd/dot_general | solution.py:37
  564.4 9.5 %fusion.74 = (f32[4,576]{1,0:T(4,128)S(1)}, f32[4,576,2304]{2,1,0:T(8,128)}) fusion(pred[576,2304]{1,0:T(8,128)(4,1)S(1)} %broadcast_compare_fusion.5, bf16[2304,4,128]{2,0,1:T(8,128)(2,1)S(1)} %get-tuple-element.328, bf16[1,576,4,128]{3,2,1,0:T(4,128)(2,1)S(1)} %constant_dynamic-slice_fusion.5), kind=kOutput, calls=%fused_computation.22.clone.1 | convolution fusion | flops 1374877440 | bytes 25519104 | tf_op jit(solution)/shard_map/while/body/eval_jaxpr/qhd,khd->hqk/dot_general | solution.py:29
  574.0 10.6 %fusion.75 = f32[4,576]{1,0:T(4,128)S(1)} fusion(f32[4,576,2304]{2,1,0:T(8,128)} %get-tuple-element.306, f32[4,576]{1,0:T(4,128)S(1)} %get-tuple-element.307, pred[576,2304]{1,0:T(8,128)(4,1)S(1)} %broadcast_compare_fusion.5), kind=kLoop, calls=%fused_computation.23.clone.1 | loop fusion | flops 21231360 | bytes 22579200 | tf_op jit(solution)/shard_map/while/body/eval_jaxpr/reduce_sum | solution.py:36
  584.6 10.4 %fusion.76 = bf16[4,576,4,128]{3,1,0,2:T(8,128)(2,1)} fusion(bf16[4,576,4,128]{3,1,0,2:T(8,128)(2,1)} %get-tuple-element.317, s32[]{:T(128)} %get-tuple-element.316, bf16[2304,4,128]{2,0,1:T(8,128)(2,1)S(1)} %copy-done.2, f32[4,576,2304]{2,1,0:T(8,128)} %get-tuple-element.306, f32[4,576]{1,0:T(4,128)S(1)} %get-tuple-element.307, ...), kind=kOutput, calls=%fused_computation.31.clone.1 | convolution fusion | flops 1380777984 | bytes 25528832 | tf_op jit(solution)/shard_map/while/body/eval_jaxpr/hqk,khd->qhd/dot_general | solution.py:37
  598.0 9.5 %fusion.74 = (f32[4,576]{1,0:T(4,128)S(1)}, f32[4,576,2304]{2,1,0:T(8,128)}) fusion(pred[576,2304]{1,0:T(8,128)(4,1)S(1)} %broadcast_compare_fusion.5, bf16[2304,4,128]{2,0,1:T(8,128)(2,1)S(1)} %get-tuple-element.328, bf16[1,576,4,128]{3,2,1,0:T(4,128)(2,1)S(1)} %constant_dynamic-slice_fusion.5), kind=kOutput, calls=%fused_computation.22.clone.1 | convolution fusion | flops 1374877440 | bytes 25519104 | tf_op jit(solution)/shard_map/while/body/eval_jaxpr/qhd,khd->hqk/dot_general | solution.py:29
  607.6 10.6 %fusion.75 = f32[4,576]{1,0:T(4,128)S(1)} fusion(f32[4,576,2304]{2,1,0:T(8,128)} %get-tuple-element.306, f32[4,576]{1,0:T(4,128)S(1)} %get-tuple-element.307, pred[576,2304]{1,0:T(8,128)(4,1)S(1)} %broadcast_compare_fusion.5), kind=kLoop, calls=%fused_computation.23.clone.1 | loop fusion | flops 21231360 | bytes 22579200 | tf_op jit(solution)/shard_map/while/body/eval_jaxpr/reduce_sum | solution.py:36
  618.3 10.4 %fusion.76 = bf16[4,576,4,128]{3,1,0,2:T(8,128)(2,1)} fusion(bf16[4,576,4,128]{3,1,0,2:T(8,128)(2,1)} %get-tuple-element.317, s32[]{:T(128)} %get-tuple-element.316, bf16[2304,4,128]{2,0,1:T(8,128)(2,1)S(1)} %copy-done.2, f32[4,576,2304]{2,1,0:T(8,128)} %get-tuple-element.306, f32[4,576]{1,0:T(4,128)S(1)} %get-tuple-element.307, ...), kind=kOutput, calls=%fused_computation.31.clone.1 | convolution fusion | flops 1380777984 | bytes 25528832 | tf_op jit(solution)/shard_map/while/body/eval_jaxpr/hqk,khd->qhd/dot_general | solution.py:37
  631.7 9.5 %fusion.74 = (f32[4,576]{1,0:T(4,128)S(1)}, f32[4,576,2304]{2,1,0:T(8,128)}) fusion(pred[576,2304]{1,0:T(8,128)(4,1)S(1)} %broadcast_compare_fusion.5, bf16[2304,4,128]{2,0,1:T(8,128)(2,1)S(1)} %get-tuple-element.328, bf16[1,576,4,128]{3,2,1,0:T(4,128)(2,1)S(1)} %constant_dynamic-slice_fusion.5), kind=kOutput, calls=%fused_computation.22.clone.1 | convolution fusion | flops 1374877440 | bytes 25519104 | tf_op jit(solution)/shard_map/while/body/eval_jaxpr/qhd,khd->hqk/dot_general | solution.py:29
  641.2 10.6 %fusion.75 = f32[4,576]{1,0:T(4,128)S(1)} fusion(f32[4,576,2304]{2,1,0:T(8,128)} %get-tuple-element.306, f32[4,576]{1,0:T(4,128)S(1)} %get-tuple-element.307, pred[576,2304]{1,0:T(8,128)(4,1)S(1)} %broadcast_compare_fusion.5), kind=kLoop, calls=%fused_computation.23.clone.1 | loop fusion | flops 21231360 | bytes 22579200 | tf_op jit(solution)/shard_map/while/body/eval_jaxpr/reduce_sum | solution.py:36
  651.9 10.4 %fusion.76 = bf16[4,576,4,128]{3,1,0,2:T(8,128)(2,1)} fusion(bf16[4,576,4,128]{3,1,0,2:T(8,128)(2,1)} %get-tuple-element.317, s32[]{:T(128)} %get-tuple-element.316, bf16[2304,4,128]{2,0,1:T(8,128)(2,1)S(1)} %copy-done.2, f32[4,576,2304]{2,1,0:T(8,128)} %get-tuple-element.306, f32[4,576]{1,0:T(4,128)S(1)} %get-tuple-element.307, ...), kind=kOutput, calls=%fused_computation.31.clone.1 | convolution fusion | flops 1380777984 | bytes 25528832 | tf_op jit(solution)/shard_map/while/body/eval_jaxpr/hqk,khd->qhd/dot_general | solution.py:37
  662.3 2.8 pad_maximum_fusion.3
  665.1 12.0 %copy.35 = bf16[2,2304,4,128]{3,2,1,0:T(4,128)(2,1)} copy(bf16[2,2304,4,128]{3,1,2,0:T(8,128)(2,1)S(1)} %pad_maximum_fusion.3) | data formatting | bytes 9437184 | tf_op jit(solution)/shard_map/stack | solution.py:67
  677.1 8.0 reshape.108
  687.3 2.5 collective-permute-done.2
  690.1 56.5 %all_to_all.24 = bf16[96,48,512]{2,1,0:T(8,128)(2,1)S(1)} all-to-all(bf16[96,48,512]{2,1,0:T(8,128)(2,1)S(1)} %pad_maximum_fusion.4), channel_id=1, replica_groups=mesh['win'=16,'head'=2] {'head'}, dimensions={0} | all-to-all | bytes 9437184 | tf_op jit(solution)/shard_map/all_to_all | solution.py:89
  748.2 55.7 %collective-permute-done.3 = bf16[48,24,1024]{2,1,0:T(8,128)(2,1)S(1)} collective-permute-done((bf16[48,24,1024]{2,1,0:T(8,128)(2,1)S(1)}, bf16[48,24,1024]{2,1,0:T(8,128)(2,1)S(1)}, u32[]{:S(2)}, u32[]{:S(2)}) %collective-permute-start.3) | collective-permute-done | bytes 2359328 | tf_op jit(solution)/shard_map/ppermute | solution.py:12
  803.9 2.7 maximum_bitcast_fusion
  (83 shorter events, 37.4 us)
Async XLA Ops:
  6.1 157.7 %collective-permute-start = (bf16[3,48,24,1024]{3,2,1,0:T(8,128)(2,1)S(1)}, bf16[3,48,24,1024]{3,2,1,0:T(8,128)(2,1)S(1)}, u32[]{:S(2)}, u32[]{:S(2)}) collective-permute-start(bf16[3,48,24,1024]{3,2,1,0:T(8,128)(2,1)S(1)} %get-tuple-element.207), channel_id=1, source_target_pairs={{0,28},{2,30},{4,0},{6,2},{8,4},{10,6},{12,8},{14,10},{16,12},{18,... | collective-permute-start | bytes 21233672 | tf_op jit(solution)/shard_map/ppermute | solution.py:12
  326.8 5.1 copy-start
  333.9 12.4 %collective-permute-start.1 = (bf16[3,24,48,512]{3,2,1,0:T(8,128)(2,1)}, bf16[3,24,48,512]{3,2,1,0:T(8,128)(2,1)S(1)}, u32[]{:S(2)}, u32[]{:S(2)}) collective-permute-start(bf16[3,24,48,512]{3,2,1,0:T(8,128)(2,1)} %slice.95), channel_id=1, source_target_pairs={{0,2},{2,0},{4,6},{6,4},{8,10},{10,8},{12,14},{14,12},{16,18},{18,... | collective-permute-start | bytes 10616840 | tf_op jit(solution)/shard_map/ppermute | solution.py:18
  401.9 10.7 %copy-start.3 = (bf16[2304,4,128]{2,0,1:T(8,128)(2,1)S(1)}, bf16[2304,4,128]{2,0,1:T(8,128)(2,1)}, u32[]{:S(2)}) copy-start(bf16[2304,4,128]{2,0,1:T(8,128)(2,1)} %get-tuple-element.353) | copy-start | bytes 7077892 | tf_op jit(solution)/shard_map/while
  434.8 10.7 %copy-start.3 = (bf16[2304,4,128]{2,0,1:T(8,128)(2,1)S(1)}, bf16[2304,4,128]{2,0,1:T(8,128)(2,1)}, u32[]{:S(2)}) copy-start(bf16[2304,4,128]{2,0,1:T(8,128)(2,1)} %get-tuple-element.353) | copy-start | bytes 7077892 | tf_op jit(solution)/shard_map/while
  467.8 10.7 %copy-start.3 = (bf16[2304,4,128]{2,0,1:T(8,128)(2,1)S(1)}, bf16[2304,4,128]{2,0,1:T(8,128)(2,1)}, u32[]{:S(2)}) copy-start(bf16[2304,4,128]{2,0,1:T(8,128)(2,1)} %get-tuple-element.353) | copy-start | bytes 7077892 | tf_op jit(solution)/shard_map/while
  500.7 10.7 %copy-start.3 = (bf16[2304,4,128]{2,0,1:T(8,128)(2,1)S(1)}, bf16[2304,4,128]{2,0,1:T(8,128)(2,1)}, u32[]{:S(2)}) copy-start(bf16[2304,4,128]{2,0,1:T(8,128)(2,1)} %get-tuple-element.353) | copy-start | bytes 7077892 | tf_op jit(solution)/shard_map/while
  521.8 2.4 copy-start.1
  521.8 6.0 copy-start.4
  540.4 10.7 %copy-start.2 = (bf16[2304,4,128]{2,0,1:T(8,128)(2,1)S(1)}, bf16[2304,4,128]{2,0,1:T(8,128)(2,1)}, u32[]{:S(2)}) copy-start(bf16[2304,4,128]{2,0,1:T(8,128)(2,1)} %get-tuple-element.329) | copy-start | bytes 7077892 | tf_op jit(solution)/shard_map/while
  574.0 10.7 %copy-start.2 = (bf16[2304,4,128]{2,0,1:T(8,128)(2,1)S(1)}, bf16[2304,4,128]{2,0,1:T(8,128)(2,1)}, u32[]{:S(2)}) copy-start(bf16[2304,4,128]{2,0,1:T(8,128)(2,1)} %get-tuple-element.329) | copy-start | bytes 7077892 | tf_op jit(solution)/shard_map/while
  607.6 10.7 %copy-start.2 = (bf16[2304,4,128]{2,0,1:T(8,128)(2,1)S(1)}, bf16[2304,4,128]{2,0,1:T(8,128)(2,1)}, u32[]{:S(2)}) copy-start(bf16[2304,4,128]{2,0,1:T(8,128)(2,1)} %get-tuple-element.329) | copy-start | bytes 7077892 | tf_op jit(solution)/shard_map/while
  641.2 10.7 %copy-start.2 = (bf16[2304,4,128]{2,0,1:T(8,128)(2,1)S(1)}, bf16[2304,4,128]{2,0,1:T(8,128)(2,1)}, u32[]{:S(2)}) copy-start(bf16[2304,4,128]{2,0,1:T(8,128)(2,1)} %get-tuple-element.329) | copy-start | bytes 7077892 | tf_op jit(solution)/shard_map/while
  685.2 4.5 slice-start
  686.7 3.0 collective-permute-start.2
  747.8 56.1 %collective-permute-start.3 = (bf16[48,24,1024]{2,1,0:T(8,128)(2,1)S(1)}, bf16[48,24,1024]{2,1,0:T(8,128)(2,1)S(1)}, u32[]{:S(2)}, u32[]{:S(2)}) collective-permute-start(bf16[48,24,1024]{2,1,0:T(8,128)(2,1)S(1)} %get-tuple-element.208), channel_id=1, source_target_pairs={{0,4},{2,6},{4,8},{6,10},{8,12},{10,14},{12,16},{14,18},{16,20},{1... | collective-permute-start | bytes 7077896 | tf_op jit(solution)/shard_map/ppermute | solution.py:12
